TPU v7x, 32 devices: a whole 2x2x4 slice. The times are simulated.
32 devices in a mesh: section: 2 (over y), dp: 8 (over z, core), vocab: 2 (over x).
Axes of the slice: x: 2, y: 2, z: 4, core: 2. Of those that a mesh axis runs over, the one named last changes fastest.
Arguments:
- activations: bfloat16 [2, 1024, 2048], P('section', 'dp'), may hold values from -32 to 32
- token_ids: int32 [2, 1024], replicated, may hold values from 0 to 8191
- embed_table: bfloat16 [8192, 2048], P(('dp', 'vocab')), may hold values from -3 to 3
Outputs:
- tied_grad: bfloat16 [16, 2, 256, 2048], P(('dp', 'vocab'), 'section')
All inputs are finite; a program needn't handle non-finite values.
Results may differ from a plain program's by a relative error of at most 0.0029.
Values may be sent and summed in bfloat16 or wider, within the bound.
A program may use at most 128 MiB of HBM per device.

v0:
```python
import jax
import jax.numpy as jnp
from jax import lax
from jax.sharding import PartitionSpec as P


def from_partner(block, axis, apart):
    count = lax.axis_size(axis)
    route = []
    for low in range(count):
        high = low | 1 << apart
        if high != low and high < count:
            route += [(low, high), (high, low)]
    return lax.ppermute(block, axis, route)


def spread_rows(row_tuple):
    return (
        lax.all_gather(row_tuple[0], "dp", axis=0, tiled=True),
        lax.all_gather(row_tuple[1], "dp", axis=0, tiled=True),
    )


def local_stats(logits):
    row_peak = jnp.max(logits, axis=1)
    row_total = jnp.sum(jnp.exp(logits - row_peak[:, None]), axis=1)
    return (row_peak, row_total)


def body(activations, token_ids, embed_table):
    own_rows = activations[0]
    model_width = own_rows.shape[1]
    table_count = embed_table.shape[0]
    section_index = lax.axis_index("section")
    half_rows = table_count // lax.axis_size("section")
    block_first = (
        lax.axis_index("dp") * lax.axis_size("vocab") + lax.axis_index("vocab")
    ) * table_count
    partner = from_partner(own_rows, "section", 0)
    cot_rows = jnp.where(section_index == 0, own_rows, partner)
    hid_rows = jnp.where(section_index == 0, partner, own_rows)
    cot_all, hid_all = spread_rows((cot_rows, hid_rows))
    my_table = lax.dynamic_slice_in_dim(embed_table, section_index * half_rows, half_rows, 0)
    row_first = block_first + section_index * half_rows
    positions = jnp.arange(half_rows, dtype=jnp.int32)[None, :]
    target_hot = (token_ids[1] - row_first)[:, None] == positions
    input_hot = (token_ids[0] - row_first)[:, None] == positions
    logits = lax.dot_general(
        hid_all, my_table, (((1,), (1,)), ((), ())), preferred_element_type=jnp.float32
    )
    row_peak, row_total = local_stats(logits)
    peak_all = lax.pmax(row_peak, ("section", "dp", "vocab"))
    total_all = lax.psum(row_total * jnp.exp(row_peak - peak_all), ("section", "dp", "vocab"))
    probs = jnp.exp(logits - peak_all[:, None]) / total_all[:, None]
    last_part = (probs - target_hot.astype(jnp.float32)).astype(jnp.bfloat16)
    first_part = input_hot.astype(jnp.bfloat16)
    summed = lax.dot_general(
        last_part, hid_all, (((0,), (0,)), ((), ())), preferred_element_type=jnp.float32
    )
    summed = summed + lax.dot_general(
        first_part, cot_all, (((0,), (0,)), ((), ())), preferred_element_type=jnp.float32
    )
    return summed.astype(jnp.bfloat16).reshape(1, 1, half_rows, model_width)


def solution(mesh):
    return jax.shard_map(
        body,
        mesh=mesh,
        in_specs=(P("section", "dp", None), P(), P(("dp", "vocab"), None)),
        out_specs=P(("dp", "vocab"), "section", None, None),
        check_vma=False,
    )
```

profile of v0, /device:TPU:0, one launch (start us, length us, event | category | flops | bytes accessed | tf_op | source)
XLA Modules:
  0.0 170.4 jit_solution(3358210218269821049)
XLA Ops:
  6.5 0.0 copy-start
  6.5 0.0 all-gather.3.cloned.1.call-start
  6.5 3.0 %collective-permute-start = (bf16[128,2048]{1,0:T(8,128)(2,1)}, bf16[128,2048]{1,0:T(8,128)(2,1)S(1)}, u32[]{:S(2)}, u32[]{:S(2)}) collective-permute-start(bf16[128,2048]{1,0:T(8,128)(2,1)} %bitcast.10), channel_id=1, source_target_pairs={{0,16},{16,0},{1,17},{17,1},{2,18},{18,2},{3,19},{19,3},{4,20},{20... | collective-permute-start | bytes 1572872 | tf_op jit(solution)/shard_map/ppermute | solution.py:14
  9.5 12.1 %collective-permute-done = bf16[128,2048]{1,0:T(8,128)(2,1)S(1)} collective-permute-done((bf16[128,2048]{1,0:T(8,128)(2,1)}, bf16[128,2048]{1,0:T(8,128)(2,1)S(1)}, u32[]{:S(2)}, u32[]{:S(2)}) %collective-permute-start) | collective-permute-done | bytes 524320 | tf_op jit(solution)/shard_map/ppermute | solution.py:14
  21.7 2.1 %broadcast_select_fusion.1 = (bf16[128,2048]{1,0:T(8,128)(2,1)}, bf16[128,2048]{1,0:T(8,128)(2,1)}) fusion(bf16[128,2048]{1,0:T(8,128)(2,1)S(1)} %collective-permute-done, pred[]{:T(512)S(6)} %eq.14, bf16[1,128,2048]{2,1,0:T(8,128)(2,1)} %param.3), kind=kLoop, calls=%fused_computation.15 | loop fusion | flops 524288 | bytes 2097153 | tf_op jit(solution)/shard_map/jit(_where)/select_n | solution.py:41
  23.8 0.0 all-gather.3.cloned.1.call-update
  23.8 0.0 all-gather.5.cloned.1.call-start
  23.9 0.7 all-gather.5.cloned.1.call-update
  24.6 0.8 slice_subtract_fusion.1
  25.4 46.9 %all-gather.3.cloned.1.call-done = bf16[1024,2048]{1,0:T(8,128)(2,1)} async-done(((bf16[128,2048]{1,0:T(8,128)(2,1)}), bf16[1024,2048]{1,0:T(8,128)(2,1)}) %all-gather.3.cloned.1.call-update) | async-done | bytes 4194320 | tf_op jit(solution)/shard_map/all_gather | solution.py:20
  72.3 0.0 copy-done
  72.3 3.5 %fusion.10 = (f32[1024]{0:T(1024)S(1)}, f32[1024,256]{0,1:T(8,128)S(1)}) fusion(bf16[1024,2048]{1,0:T(8,128)(2,1)} %all-gather.3.cloned.1.call-done, bf16[512,2048]{1,0:T(8,128)(2,1)S(1)} %copy-done, s32[]{:T(128)S(6)} %select_n.17), kind=kOutput, calls=%fused_computation.20 | convolution fusion | flops 1074002944 | bytes 6295556 | tf_op jit(solution)/shard_map/dot_general | solution.py:48
  75.8 42.2 %pmax.7 = f32[1024]{0:T(1024)S(1)} all-reduce(f32[1024]{0:T(1024)S(1)} %get-tuple-element.9), channel_id=1, replica_groups=mesh['section'=2,'dp'=8,'vocab'=2] {'section','dp','vocab'}, use_global_device_ids=true, to_apply=%region_1.2 | all-reduce | flops 1024 | bytes 8192 | tf_op jit(solution)/shard_map/pmax | solution.py:52
  118.0 0.2 exponential_reduce_fusion
  118.2 39.3 %psum.7 = f32[1024]{0:T(1024)S(1)} all-reduce(f32[1024]{0:T(1024)S(1)} %exponential_multiply_fusion), channel_id=1, replica_groups=mesh['section'=2,'dp'=8,'vocab'=2] {'section','dp','vocab'}, use_global_device_ids=true, to_apply=%region_3.4 | all-reduce | flops 1024 | bytes 8192 | tf_op jit(solution)/shard_map/psum | solution.py:53
  157.5 0.0 all-gather.5.cloned.1.call-done
  157.5 0.0 copy-start.1
  157.5 3.7 %fusion.4 = f32[256,2048]{1,0:T(8,128)S(1)} fusion(bf16[1024,2048]{1,0:T(8,128)(2,1)} %all-gather.5.cloned.1.call-done, s32[1024]{0:T(1024)S(1)} %bitcast.12), kind=kOutput, calls=%fused_computation.9 | convolution fusion | flops 1074003968 | bytes 6295552 | tf_op jit(solution)/shard_map/dot_general | solution.py:60
  161.2 0.0 copy-done.1
  161.2 2.3 %fusion.1 = bf16[1,1,256,2048]{3,2,1,0:T(8,128)(2,1)} fusion(f32[256,2048]{1,0:T(8,128)S(1)} %fusion.4, bf16[1024,2048]{1,0:T(8,128)(2,1)S(1)} %copy-done.1, f32[1024,256]{0,1:T(8,128)S(1)} %get-tuple-element.10, s32[1024]{0:T(1024)S(1)} %bitcast.11, f32[1024]{0:T(1024)S(1)} %psum.7, f32[1024]{0:T(1024)S(1)} %pmax.7), kind=kOutput, calls=%fused_computation.2 | convolution fusion | flops 1076363264 | bytes 8400896 | tf_op jit(solution)/shard_map/dot_general | solution.py:57
  (1 shorter events, 0.0 us)
Async XLA Ops:
  6.5 65.8 %copy-start = (bf16[512,2048]{1,0:T(8,128)(2,1)S(1)}, bf16[512,2048]{1,0:T(8,128)(2,1)}, u32[]{:S(2)}) copy-start(bf16[512,2048]{1,0:T(8,128)(2,1)} %param.5) | copy-start | bytes 6291460
  6.5 65.8 %all-gather.3.cloned.1.call-start = ((), (), s32[]{:S(2)}) async-start(), calls=%async_computation | async-start | bytes 4718592 | tf_op jit(solution)/shard_map/all_gather | solution.py:20
  6.5 15.1 %collective-permute-start = (bf16[128,2048]{1,0:T(8,128)(2,1)}, bf16[128,2048]{1,0:T(8,128)(2,1)S(1)}, u32[]{:S(2)}, u32[]{:S(2)}) collective-permute-start(bf16[128,2048]{1,0:T(8,128)(2,1)} %bitcast.10), channel_id=1, source_target_pairs={{0,16},{16,0},{1,17},{17,1},{2,18},{18,2},{3,19},{19,3},{4,20},{20... | collective-permute-start | bytes 1572872 | tf_op jit(solution)/shard_map/ppermute | solution.py:14
  23.8 133.7 %all-gather.5.cloned.1.call-start = ((), (), s32[]{:S(2)}) async-start(), calls=%async_computation.1 | async-start | bytes 4718592 | tf_op jit(solution)/shard_map/all_gather | solution.py:19
  157.5 3.7 %copy-start.1 = (bf16[1024,2048]{1,0:T(8,128)(2,1)S(1)}, bf16[1024,2048]{1,0:T(8,128)(2,1)}, u32[]{:S(2)}) copy-start(bf16[1024,2048]{1,0:T(8,128)(2,1)} %all-gather.3.cloned.1.call-done) | copy-start | bytes 12582916
Sparse Core Ops, SparseCore 0:
  23.9 48.3 all-gather.2
  73.9 46.7 all-gather.4
where the time goes:
time: 171 us; the launch traced here: 170 us
  blocking collectives  81.5 us (48%)
  waiting for transfers between devices  59.8 us (35%)
  between operations  13.4 us (8%)
  matrix products  9.52 us (6%)
  other arithmetic  3.09 us (2%)
  starting transfers between devices  3.04 us (2%)
    all_gather x1, waiting for transfers between devices, spread_rows(): lax.all_gather(row_tuple[1], 'dp', axis=0, tiled=True)  46.9 us
    pmax x1, blocking collectives, body(): peak_all = lax.pmax(row_peak, ('section', 'dp', 'vocab'))  42.2 us
    psum x1, blocking collectives, body(): lax.psum(row_total * jnp.exp(row_peak - peak_all), ('section', 'dp', 'voc...  39.3 us
    ppermute x1, waiting for transfers between devices, from_partner(): return lax.ppermute(block, axis, route)  12.1 us
    dot_general x1, matrix products, body(): lax.dot_general(first_part, cot_all, (((0,), (0,)), ((), ())), preferred_...  3.7 us
    dot_general x1, matrix products, body(): lax.dot_general(hid_all, my_table, (((1,), (1,)), ((), ())), preferred_el...  3.48 us
  transfers between devices with their start and end apart: 3, of which 2 were waited for; matrix products, arithmetic and copies ran while one was open for 3% of the time, Pallas kernels for 0%

commit v1 on v0

--- a/solution.py
+++ b/solution.py
@@ -50,7 +50,9 @@
     )
     row_peak, row_total = local_stats(logits)
     peak_all = lax.pmax(row_peak, ("section", "dp", "vocab"))
-    total_all = lax.psum(row_total * jnp.exp(row_peak - peak_all), ("section", "dp", "vocab"))
+    total_all = jnp.sum(
+        lax.all_gather(row_total * jnp.exp(row_peak - peak_all), ("section", "dp", "vocab")), axis=0
+    )
     probs = jnp.exp(logits - peak_all[:, None]) / total_all[:, None]
     last_part = (probs - target_hot.astype(jnp.float32)).astype(jnp.bfloat16)
     first_part = input_hot.astype(jnp.bfloat16)

time: 171 us -> 198 us (1.16)
  blocking collectives: 81.5 us -> 108 us
    all_gather x0 -> x1, blocking collectives: none -> 66.2 us  [body(): lax.all_gather(row_total * jnp.exp(row_peak - peak_all), ('section', 'dp'...]
    psum x1 -> x0, blocking collectives: 39.3 us -> none  [body(): lax.psum(row_total * jnp.exp(row_peak - peak_all), ('section', 'dp', 'voc...]
  transfers between devices with their start and end apart: 3 -> 3, of which waited for: 2 -> 2; matrix products, arithmetic and copies ran while one was open for 3% -> 2% of each run, Pallas kernels for 0% -> 0%
where the time goes in v1:
time: 198 us; the launch traced here: 197 us
  blocking collectives  108 us (55%)
  waiting for transfers between devices  59.8 us (30%)
  between operations  13.5 us (7%)
  matrix products  9.51 us (5%)
  other arithmetic  3.12 us (2%)
  starting transfers between devices  3.04 us (2%)
    all_gather x1, blocking collectives, body(): lax.all_gather(row_total * jnp.exp(row_peak - peak_all), ('section', 'dp'...  66.2 us
    all_gather x1, waiting for transfers between devices, spread_rows(): lax.all_gather(row_tuple[1], 'dp', axis=0, tiled=True)  46.9 us
    pmax x1, blocking collectives, body(): peak_all = lax.pmax(row_peak, ('section', 'dp', 'vocab'))  42.2 us
    ppermute x1, waiting for transfers between devices, from_partner(): return lax.ppermute(block, axis, route)  12.1 us
  transfers between devices with their start and end apart: 3, of which 2 were waited for; matrix products, arithmetic and copies ran while one was open for 2% of the time, Pallas kernels for 0%

profile of v1, /device:TPU:0, one launch (start us, length us, event | category | flops | bytes accessed | tf_op | source)
XLA Modules:
  0.0 197.4 jit_solution(2147089327923260972)
XLA Ops:
  6.5 0.0 copy-start
  6.5 0.0 all-gather.4.cloned.1.call-start
  6.5 3.0 %collective-permute-start = (bf16[128,2048]{1,0:T(8,128)(2,1)}, bf16[128,2048]{1,0:T(8,128)(2,1)S(1)}, u32[]{:S(2)}, u32[]{:S(2)}) collective-permute-start(bf16[128,2048]{1,0:T(8,128)(2,1)} %bitcast.10), channel_id=1, source_target_pairs={{0,16},{16,0},{1,17},{17,1},{2,18},{18,2},{3,19},{19,3},{4,20},{20... | collective-permute-start | bytes 1572872 | tf_op jit(solution)/shard_map/ppermute | solution.py:14
  9.5 12.1 %collective-permute-done = bf16[128,2048]{1,0:T(8,128)(2,1)S(1)} collective-permute-done((bf16[128,2048]{1,0:T(8,128)(2,1)}, bf16[128,2048]{1,0:T(8,128)(2,1)S(1)}, u32[]{:S(2)}, u32[]{:S(2)}) %collective-permute-start) | collective-permute-done | bytes 524320 | tf_op jit(solution)/shard_map/ppermute | solution.py:14
  21.7 2.1 %broadcast_select_fusion.1 = (bf16[128,2048]{1,0:T(8,128)(2,1)}, bf16[128,2048]{1,0:T(8,128)(2,1)}) fusion(bf16[128,2048]{1,0:T(8,128)(2,1)S(1)} %collective-permute-done, pred[]{:T(512)S(6)} %eq.14, bf16[1,128,2048]{2,1,0:T(8,128)(2,1)} %param.3), kind=kLoop, calls=%fused_computation.15 | loop fusion | flops 524288 | bytes 2097153 | tf_op jit(solution)/shard_map/jit(_where)/select_n | solution.py:41
  23.8 0.0 all-gather.4.cloned.1.call-update
  23.8 0.0 all-gather.6.cloned.1.call-start
  23.9 0.7 all-gather.6.cloned.1.call-update
  24.6 0.8 slice_subtract_fusion.1
  25.4 46.9 %all-gather.4.cloned.1.call-done = bf16[1024,2048]{1,0:T(8,128)(2,1)} async-done(((bf16[128,2048]{1,0:T(8,128)(2,1)}), bf16[1024,2048]{1,0:T(8,128)(2,1)}) %all-gather.4.cloned.1.call-update) | async-done | bytes 4194320 | tf_op jit(solution)/shard_map/all_gather | solution.py:20
  72.3 0.0 copy-done
  72.3 3.5 %fusion.10 = (f32[1024]{0:T(1024)S(1)}, f32[1024,256]{0,1:T(8,128)S(1)}) fusion(bf16[1024,2048]{1,0:T(8,128)(2,1)} %all-gather.4.cloned.1.call-done, bf16[512,2048]{1,0:T(8,128)(2,1)S(1)} %copy-done, s32[]{:T(128)S(6)} %select_n.17), kind=kOutput, calls=%fused_computation.20 | convolution fusion | flops 1074002944 | bytes 6295556 | tf_op jit(solution)/shard_map/dot_general | solution.py:48
  75.8 42.2 %pmax.7 = f32[1024]{0:T(1024)S(1)} all-reduce(f32[1024]{0:T(1024)S(1)} %get-tuple-element.9), channel_id=1, replica_groups=mesh['section'=2,'dp'=8,'vocab'=2] {'section','dp','vocab'}, use_global_device_ids=true, to_apply=%region_1.2 | all-reduce | flops 1024 | bytes 8192 | tf_op jit(solution)/shard_map/pmax | solution.py:52
  118.0 0.2 exponential_reduce_fusion
  118.2 66.2 %all-gather = f32[32768]{0:T(1024)S(1)} all-gather(f32[1024]{0:T(1024)S(1)} %exponential_multiply_fusion), channel_id=2, replica_groups=mesh['section'=2,'dp'=8,'vocab'=2] {'section','dp','vocab'}, dimensions={0}, use_global_device_ids=true | all-gather | bytes 135168 | tf_op jit(solution)/shard_map/all_gather | solution.py:54
  184.5 0.0 all-gather.6.cloned.1.call-done
  184.5 0.0 copy-start.1
  184.5 3.7 %fusion.4 = f32[256,2048]{1,0:T(8,128)S(1)} fusion(bf16[1024,2048]{1,0:T(8,128)(2,1)} %all-gather.6.cloned.1.call-done, s32[1024]{0:T(1024)S(1)} %bitcast.12), kind=kOutput, calls=%fused_computation.9 | convolution fusion | flops 1074003968 | bytes 6295552 | tf_op jit(solution)/shard_map/dot_general | solution.py:62
  188.2 0.0 copy-done.1
  188.2 2.3 %fusion.1 = bf16[1,1,256,2048]{3,2,1,0:T(8,128)(2,1)} fusion(f32[256,2048]{1,0:T(8,128)S(1)} %fusion.4, bf16[1024,2048]{1,0:T(8,128)(2,1)S(1)} %copy-done.1, f32[1024,256]{0,1:T(8,128)S(1)} %get-tuple-element.10, s32[1024]{0:T(1024)S(1)} %bitcast.11, f32[1024]{0:T(1024)S(1)} %reduce_sum.19, f32[1024]{0:T(1024)S(1)} %pmax.7), kind=kOutput, calls=%fused_computation.2 | convolution fusion | flops 1076363264 | bytes 8400896 | tf_op jit(solution)/shard_map/dot_general | solution.py:59
  (3 shorter events, 0.1 us)
Async XLA Ops:
  6.5 65.8 %copy-start = (bf16[512,2048]{1,0:T(8,128)(2,1)S(1)}, bf16[512,2048]{1,0:T(8,128)(2,1)}, u32[]{:S(2)}) copy-start(bf16[512,2048]{1,0:T(8,128)(2,1)} %param.5) | copy-start | bytes 6291460
  6.5 65.8 %all-gather.4.cloned.1.call-start = ((), (), s32[]{:S(2)}) async-start(), calls=%async_computation | async-start | bytes 4718592 | tf_op jit(solution)/shard_map/all_gather | solution.py:20
  6.5 15.1 %collective-permute-start = (bf16[128,2048]{1,0:T(8,128)(2,1)}, bf16[128,2048]{1,0:T(8,128)(2,1)S(1)}, u32[]{:S(2)}, u32[]{:S(2)}) collective-permute-start(bf16[128,2048]{1,0:T(8,128)(2,1)} %bitcast.10), channel_id=1, source_target_pairs={{0,16},{16,0},{1,17},{17,1},{2,18},{18,2},{3,19},{19,3},{4,20},{20... | collective-permute-start | bytes 1572872 | tf_op jit(solution)/shard_map/ppermute | solution.py:14
  23.8 160.7 %all-gather.6.cloned.1.call-start = ((), (), s32[]{:S(2)}) async-start(), calls=%async_computation.1 | async-start | bytes 4718592 | tf_op jit(solution)/shard_map/all_gather | solution.py:19
  184.5 3.7 %copy-start.1 = (bf16[1024,2048]{1,0:T(8,128)(2,1)S(1)}, bf16[1024,2048]{1,0:T(8,128)(2,1)}, u32[]{:S(2)}) copy-start(bf16[1024,2048]{1,0:T(8,128)(2,1)} %all-gather.4.cloned.1.call-done) | copy-start | bytes 12582916
Sparse Core Ops, SparseCore 0:
  23.9 48.3 all-gather.3
  73.9 46.7 all-gather.5

commit v2 on v0

--- a/solution.py
+++ b/solution.py
@@ -50,7 +50,9 @@
     )
     row_peak, row_total = local_stats(logits)
     peak_all = lax.pmax(row_peak, ("section", "dp", "vocab"))
-    total_all = lax.psum(row_total * jnp.exp(row_peak - peak_all), ("section", "dp", "vocab"))
+    total_all = lax.psum(
+        lax.psum(row_total * jnp.exp(row_peak - peak_all), ("dp", "vocab")), "section"
+    )
     probs = jnp.exp(logits - peak_all[:, None]) / total_all[:, None]
     last_part = (probs - target_hot.astype(jnp.float32)).astype(jnp.bfloat16)
     first_part = input_hot.astype(jnp.bfloat16)

time: 171 us -> 168 us (0.982)
  blocking collectives: 81.5 us -> 78.9 us
    psum x1 -> x2, blocking collectives: 39.3 us -> 36.7 us  [the longest x1 31.8 us: body(): lax.psum(row_total * jnp.exp(row_peak - peak_all), ('dp', 'vocab'))]
where the time goes in v2:
time: 168 us
  blocking collectives  78.9 us (47%)
  waiting for transfers between devices  59.8 us (36%)
  between operations  13.4 us (8%)
  matrix products  9.51 us (6%)
  other arithmetic  3.1 us (2%)
  starting transfers between devices  3.04 us (2%)
    all_gather x1, waiting for transfers between devices, spread_rows(): lax.all_gather(row_tuple[1], 'dp', axis=0, tiled=True)  46.9 us
    pmax x1, blocking collectives, body(): peak_all = lax.pmax(row_peak, ('section', 'dp', 'vocab'))  42.2 us
    psum x1, blocking collectives, body(): lax.psum(row_total * jnp.exp(row_peak - peak_all), ('dp', 'vocab'))  31.8 us
    ppermute x1, waiting for transfers between devices, from_partner(): return lax.ppermute(block, axis, route)  12.1 us
    psum x1, blocking collectives, body(): lax.psum(lax.psum(row_total * jnp.exp(row_peak - peak_all), ('dp', 'vocab...  4.93 us
    dot_general x1, matrix products, body(): lax.dot_general(first_part, cot_all, (((0,), (0,)), ((), ())), preferred_...  3.7 us
    dot_general x1, matrix products, body(): lax.dot_general(hid_all, my_table, (((1,), (1,)), ((), ())), preferred_el...  3.47 us
  transfers between devices with their start and end apart: 3, of which 2 were waited for; matrix products, arithmetic and copies ran while one was open for 3% of the time, Pallas kernels for 0%

profile of v2, /device:TPU:0, one launch (start us, length us, event | category | flops | bytes accessed | tf_op | source)
XLA Modules:
  0.0 167.8 jit_solution(1250322285658928466)
XLA Ops:
  6.5 0.0 copy-start
  6.5 0.0 all-gather.3.cloned.1.call-start
  6.5 3.0 %collective-permute-start = (bf16[128,2048]{1,0:T(8,128)(2,1)}, bf16[128,2048]{1,0:T(8,128)(2,1)S(1)}, u32[]{:S(2)}, u32[]{:S(2)}) collective-permute-start(bf16[128,2048]{1,0:T(8,128)(2,1)} %bitcast.10), channel_id=1, source_target_pairs={{0,16},{16,0},{1,17},{17,1},{2,18},{18,2},{3,19},{19,3},{4,20},{20... | collective-permute-start | bytes 1572872 | tf_op jit(solution)/shard_map/ppermute | solution.py:14
  9.5 12.1 %collective-permute-done = bf16[128,2048]{1,0:T(8,128)(2,1)S(1)} collective-permute-done((bf16[128,2048]{1,0:T(8,128)(2,1)}, bf16[128,2048]{1,0:T(8,128)(2,1)S(1)}, u32[]{:S(2)}, u32[]{:S(2)}) %collective-permute-start) | collective-permute-done | bytes 524320 | tf_op jit(solution)/shard_map/ppermute | solution.py:14
  21.7 2.1 %broadcast_select_fusion.1 = (bf16[128,2048]{1,0:T(8,128)(2,1)}, bf16[128,2048]{1,0:T(8,128)(2,1)}) fusion(bf16[128,2048]{1,0:T(8,128)(2,1)S(1)} %collective-permute-done, pred[]{:T(512)S(6)} %eq.14, bf16[1,128,2048]{2,1,0:T(8,128)(2,1)} %param.3), kind=kLoop, calls=%fused_computation.15 | loop fusion | flops 524288 | bytes 2097153 | tf_op jit(solution)/shard_map/jit(_where)/select_n | solution.py:41
  23.8 0.0 all-gather.3.cloned.1.call-update
  23.8 0.0 all-gather.5.cloned.1.call-start
  23.9 0.7 all-gather.5.cloned.1.call-update
  24.6 0.8 slice_subtract_fusion.1
  25.4 46.9 %all-gather.3.cloned.1.call-done = bf16[1024,2048]{1,0:T(8,128)(2,1)} async-done(((bf16[128,2048]{1,0:T(8,128)(2,1)}), bf16[1024,2048]{1,0:T(8,128)(2,1)}) %all-gather.3.cloned.1.call-update) | async-done | bytes 4194320 | tf_op jit(solution)/shard_map/all_gather | solution.py:20
  72.3 0.0 copy-done
  72.3 3.5 %fusion.10 = (f32[1024]{0:T(1024)S(1)}, f32[1024,256]{0,1:T(8,128)S(1)}) fusion(bf16[1024,2048]{1,0:T(8,128)(2,1)} %all-gather.3.cloned.1.call-done, bf16[512,2048]{1,0:T(8,128)(2,1)S(1)} %copy-done, s32[]{:T(128)S(6)} %select_n.17), kind=kOutput, calls=%fused_computation.20 | convolution fusion | flops 1074002944 | bytes 6295556 | tf_op jit(solution)/shard_map/dot_general | solution.py:48
  75.8 42.2 %pmax.7 = f32[1024]{0:T(1024)S(1)} all-reduce(f32[1024]{0:T(1024)S(1)} %get-tuple-element.9), channel_id=1, replica_groups=mesh['section'=2,'dp'=8,'vocab'=2] {'section','dp','vocab'}, use_global_device_ids=true, to_apply=%region_1.2 | all-reduce | flops 1024 | bytes 8192 | tf_op jit(solution)/shard_map/pmax | solution.py:52
  118.0 0.2 exponential_reduce_fusion
  118.2 31.8 %psum.14 = f32[1024]{0:T(1024)S(1)} all-reduce(f32[1024]{0:T(1024)S(1)} %exponential_multiply_fusion), channel_id=1, replica_groups=mesh['section'=2,'dp'=8,'vocab'=2] {'dp','vocab'}, use_global_device_ids=true, to_apply=%region_3.4 | all-reduce | flops 1024 | bytes 8192 | tf_op jit(solution)/shard_map/psum | solution.py:54
  150.0 4.9 %psum.15 = f32[1024]{0:T(1024)S(1)} all-reduce(f32[1024]{0:T(1024)S(1)} %psum.14), channel_id=1, replica_groups=mesh['section'=2,'dp'=8,'vocab'=2] {'section'}, use_global_device_ids=true, to_apply=%region_4.5 | all-reduce | flops 1024 | bytes 8192 | tf_op jit(solution)/shard_map/psum | solution.py:53
  154.9 0.0 all-gather.5.cloned.1.call-done
  154.9 0.0 copy-start.1
  154.9 3.7 %fusion.4 = f32[256,2048]{1,0:T(8,128)S(1)} fusion(bf16[1024,2048]{1,0:T(8,128)(2,1)} %all-gather.5.cloned.1.call-done, s32[1024]{0:T(1024)S(1)} %bitcast.12), kind=kOutput, calls=%fused_computation.9 | convolution fusion | flops 1074003968 | bytes 6295552 | tf_op jit(solution)/shard_map/dot_general | solution.py:62
  158.6 0.0 copy-done.1
  158.6 2.3 %fusion.1 = bf16[1,1,256,2048]{3,2,1,0:T(8,128)(2,1)} fusion(f32[256,2048]{1,0:T(8,128)S(1)} %fusion.4, bf16[1024,2048]{1,0:T(8,128)(2,1)S(1)} %copy-done.1, f32[1024,256]{0,1:T(8,128)S(1)} %get-tuple-element.10, s32[1024]{0:T(1024)S(1)} %bitcast.11, f32[1024]{0:T(1024)S(1)} %psum.15, f32[1024]{0:T(1024)S(1)} %pmax.7), kind=kOutput, calls=%fused_computation.2 | convolution fusion | flops 1076363264 | bytes 8400896 | tf_op jit(solution)/shard_map/dot_general | solution.py:59
  (1 shorter events, 0.0 us)
Async XLA Ops:
  6.5 65.8 %copy-start = (bf16[512,2048]{1,0:T(8,128)(2,1)S(1)}, bf16[512,2048]{1,0:T(8,128)(2,1)}, u32[]{:S(2)}) copy-start(bf16[512,2048]{1,0:T(8,128)(2,1)} %param.5) | copy-start | bytes 6291460
  6.5 65.8 %all-gather.3.cloned.1.call-start = ((), (), s32[]{:S(2)}) async-start(), calls=%async_computation | async-start | bytes 4718592 | tf_op jit(solution)/shard_map/all_gather | solution.py:20
  6.5 15.1 %collective-permute-start = (bf16[128,2048]{1,0:T(8,128)(2,1)}, bf16[128,2048]{1,0:T(8,128)(2,1)S(1)}, u32[]{:S(2)}, u32[]{:S(2)}) collective-permute-start(bf16[128,2048]{1,0:T(8,128)(2,1)} %bitcast.10), channel_id=1, source_target_pairs={{0,16},{16,0},{1,17},{17,1},{2,18},{18,2},{3,19},{19,3},{4,20},{20... | collective-permute-start | bytes 1572872 | tf_op jit(solution)/shard_map/ppermute | solution.py:14
  23.8 131.1 %all-gather.5.cloned.1.call-start = ((), (), s32[]{:S(2)}) async-start(), calls=%async_computation.1 | async-start | bytes 4718592 | tf_op jit(solution)/shard_map/all_gather | solution.py:19
  154.9 3.7 %copy-start.1 = (bf16[1024,2048]{1,0:T(8,128)(2,1)S(1)}, bf16[1024,2048]{1,0:T(8,128)(2,1)}, u32[]{:S(2)}) copy-start(bf16[1024,2048]{1,0:T(8,128)(2,1)} %all-gather.3.cloned.1.call-done) | copy-start | bytes 12582916
Sparse Core Ops, SparseCore 0:
  23.9 48.3 all-gather.2
  73.9 46.7 all-gather.4
